TPU v7x, 8 devices: a whole 2x2x1 slice. The times are simulated.
8 devices in a mesh: depth: 2 (over z, y), col: 2 (over x), row: 2 (over core).
Axes of the slice: x: 2, y: 2, z: 1, core: 2. Of those that a mesh axis runs over, the one named last changes fastest.
Arguments:
- a_mat: bfloat16 [4096, 4096], P('row', 'col')
- b_mat: bfloat16 [4096, 4096], P('row', 'col')
Outputs:
- output: bfloat16 [4096, 4096], P(('row', 'depth'), 'col')
All inputs are finite; a program needn't handle non-finite values.
Results may differ from a plain program's by a relative error of at most 0.001.
Values are sent between devices in bfloat16 or wider.
A program may use at most 1 GiB of HBM per device.

v0:
```python
import jax
import jax.numpy as jnp
from jax import lax
from jax.sharding import PartitionSpec as P

AXES_ALL = ("depth", "col", "row")


def skew_pairs(depth_n, col_n, row_n):
    col_ratio = row_n // col_n
    layer_steps = row_n // depth_n
    pairs_a0 = []
    pairs_a1 = []
    pairs_b = []
    for layer_idx in range(depth_n):
        for col_idx in range(col_n):
            for row_idx in range(row_n):
                target_dev = (layer_idx * col_n + col_idx) * row_n + row_idx
                start_blk = (row_idx + col_ratio * col_idx + layer_idx * layer_steps) % row_n
                coarse_blk = start_blk // col_ratio
                pairs_a0.append(((layer_idx * col_n + coarse_blk) * row_n + row_idx, target_dev))
                pairs_a1.append(((layer_idx * col_n + (coarse_blk + 1) % col_n) * row_n + row_idx, target_dev))
                pairs_b.append(((layer_idx * col_n + col_idx) * row_n + start_blk, target_dev))
    return pairs_a0, pairs_a1, pairs_b


def solution(mesh):
    depth_n = mesh.shape["depth"]
    col_n = mesh.shape["col"]
    row_n = mesh.shape["row"]
    col_ratio = row_n // col_n
    layer_steps = row_n // depth_n
    pairs_a0, pairs_a1, pairs_b = skew_pairs(depth_n, col_n, row_n)
    pairs_col = [((col_idx + 1) % col_n, col_idx) for col_idx in range(col_n)]
    pairs_row = [((row_idx + 1) % row_n, row_idx) for row_idx in range(row_n)]

    def local_mm(a_blk, b_blk):
        layer_idx = lax.axis_index("depth")
        row_idx = lax.axis_index("row")
        fine_side = a_blk.shape[0]
        a_first = lax.ppermute(a_blk, AXES_ALL, pairs_a0)
        if col_ratio > 1:
            a_second = lax.ppermute(a_blk, AXES_ALL, pairs_a1)
            a_joined = jnp.concatenate([a_first, a_second], axis=1)
            offset = ((row_idx + layer_idx * layer_steps) % col_ratio) * fine_side
            a_window = lax.dynamic_slice_in_dim(a_joined, offset, a_blk.shape[1], axis=1)
        else:
            a_window = a_first
        a_parts = [a_window[:, blk_idx * fine_side:(blk_idx + 1) * fine_side] for blk_idx in range(min(col_ratio, layer_steps))]
        b_cur = lax.ppermute(b_blk, AXES_ALL, pairs_b)
        part_sum = None
        for step_idx in range(layer_steps):
            a_cur = a_parts[step_idx]
            block_prod = jnp.dot(a_cur, b_cur, preferred_element_type=jnp.float32)
            part_sum = block_prod if part_sum is None else part_sum + block_prod
            if step_idx + col_ratio < layer_steps:
                a_parts.append(lax.ppermute(a_cur, "col", pairs_col))
            if step_idx + 1 < layer_steps:
                b_cur = lax.ppermute(b_cur, "row", pairs_row)
        c_rows = lax.psum_scatter(part_sum, "depth", scatter_dimension=0, tiled=True)
        return c_rows.astype(jnp.bfloat16)

    spec_in = P("row", "col")
    spec_out = P(("row", "depth"), "col")
    return jax.shard_map(local_mm, mesh=mesh, in_specs=(spec_in, spec_in), out_specs=spec_out, check_vma=False)
```

profile of v0, /device:TPU:1, one launch (start us, length us, event | category | flops | bytes accessed | tf_op | source)
XLA Modules:
  0.0 323.4 jit_solution(1894354475971283979)
XLA Ops:
  6.5 0.0 reduce-scatter.2.cloned.1.call-start
  6.5 3.9 %collective-permute-start = (bf16[2048,2048]{1,0:T(8,128)(2,1)}, bf16[2048,2048]{1,0:T(8,128)(2,1)S(1)}, u32[]{:S(2)}, u32[]{:S(2)}) collective-permute-start(bf16[2048,2048]{1,0:T(8,128)(2,1)} %param.2), channel_id=1, source_target_pairs={{0,0},{3,1},{2,2},{1,3},{6,4},{5,5},{4,6},{7,7}} | collective-permute-start | bytes 25165832 | tf_op jit(solution)/shard_map/ppermute | solution.py:41
  10.5 4.0 %collective-permute-start.1 = (bf16[2048,2048]{1,0:T(8,128)(2,1)}, bf16[2048,2048]{1,0:T(8,128)(2,1)S(1)}, u32[]{:S(2)}, u32[]{:S(2)}) collective-permute-start(bf16[2048,2048]{1,0:T(8,128)(2,1)} %param.3), channel_id=1, source_target_pairs={{0,0},{1,1},{3,2},{2,3},{5,4},{4,5},{6,6},{7,7}} | collective-permute-start | bytes 25165832 | tf_op jit(solution)/shard_map/ppermute | solution.py:50
  14.5 86.8 %collective-permute-done = bf16[2048,2048]{1,0:T(8,128)(2,1)S(1)} collective-permute-done((bf16[2048,2048]{1,0:T(8,128)(2,1)}, bf16[2048,2048]{1,0:T(8,128)(2,1)S(1)}, u32[]{:S(2)}, u32[]{:S(2)}) %collective-permute-start) | collective-permute-done | bytes 8388640 | tf_op jit(solution)/shard_map/ppermute | solution.py:41
  101.3 0.0 collective-permute-done.1
  101.3 20.5 %fusion = f32[2048,2048]{1,0:T(8,128)} fusion(bf16[2048,2048]{1,0:T(8,128)(2,1)S(1)} %collective-permute-done, bf16[2048,2048]{1,0:T(8,128)(2,1)S(1)} %collective-permute-done.1), kind=kOutput, calls=%fused_computation | convolution fusion | flops 17179869184 | bytes 33554432 | tf_op jit(solution)/shard_map/dot_general | solution.py:54
  121.8 0.0 reduce-scatter.2.cloned.1.call-update
  121.9 188.6 %reduce-scatter.2.cloned.1.call-done = f32[1024,2048]{1,0:T(8,128)} async-done(((f32[2048,2048]{1,0:T(8,128)}), f32[1024,2048]{1,0:T(8,128)}) %reduce-scatter.2.cloned.1.call-update) | async-done | bytes 8388624 | tf_op jit(solution)/shard_map/reduce_scatter | solution.py:60
  310.5 6.0 %convert_element_type.3 = bf16[1024,2048]{1,0:T(8,128)(2,1)} convert(f32[1024,2048]{1,0:T(8,128)} %reduce-scatter.2.cloned.1.call-done) | non-fusion elementwise | flops 2097152 | bytes 12582912 | tf_op jit(solution)/shard_map/convert_element_type | solution.py:61
Async XLA Ops:
  6.5 303.9 %reduce-scatter.2.cloned.1.call-start = ((), (), s32[]{:S(2)}) async-start(), calls=%async_computation.1 | async-start | bytes 25165824 | tf_op jit(solution)/shard_map/reduce_scatter | solution.py:60
  6.5 94.8 %collective-permute-start = (bf16[2048,2048]{1,0:T(8,128)(2,1)}, bf16[2048,2048]{1,0:T(8,128)(2,1)S(1)}, u32[]{:S(2)}, u32[]{:S(2)}) collective-permute-start(bf16[2048,2048]{1,0:T(8,128)(2,1)} %param.2), channel_id=1, source_target_pairs={{0,0},{3,1},{2,2},{1,3},{6,4},{5,5},{4,6},{7,7}} | collective-permute-start | bytes 25165832 | tf_op jit(solution)/shard_map/ppermute | solution.py:41
  10.5 90.8 %collective-permute-start.1 = (bf16[2048,2048]{1,0:T(8,128)(2,1)}, bf16[2048,2048]{1,0:T(8,128)(2,1)S(1)}, u32[]{:S(2)}, u32[]{:S(2)}) collective-permute-start(bf16[2048,2048]{1,0:T(8,128)(2,1)} %param.3), channel_id=1, source_target_pairs={{0,0},{1,1},{3,2},{2,3},{5,4},{4,5},{6,6},{7,7}} | collective-permute-start | bytes 25165832 | tf_op jit(solution)/shard_map/ppermute | solution.py:50
Sparse Core Ops, SparseCore 0:
  122.0 188.4 reduce-scatter.1
where the time goes:
time: 325 us; the launch traced here: 323 us
  waiting for transfers between devices  275 us (85%)
  matrix products  20.5 us (6%)
  between operations  13.4 us (4%)
  starting transfers between devices  7.97 us (2%)
  other arithmetic  6.05 us (2%)
    reduce_scatter x1, waiting for transfers between devices, local_mm(): lax.psum_scatter(part_sum, 'depth', scatter_dimension=0, tiled=True)  189 us
    ppermute x1, waiting for transfers between devices, local_mm(): a_first = lax.ppermute(a_blk, AXES_ALL, pairs_a0)  86.8 us
    dot_general x1, matrix products, local_mm(): block_prod = jnp.dot(a_cur, b_cur, preferred_element_type=jnp.float32)  20.5 us
  transfers between devices with their start and end apart: 3, of which 2 were waited for; matrix products, arithmetic and copies ran while one was open for 0% of the time, Pallas kernels for 0%

commit v1 on v0

v1 whole, which is shorter than its diff:
```python
import functools

import jax
import jax.numpy as jnp
from jax import lax
from jax.experimental import pallas as pl
from jax.experimental.pallas import tpu as pltpu
from jax.sharding import PartitionSpec as P

MESH = pl.DeviceIdType.MESH
CHUNKS = (256, 256, 256, 128, 64, 64)
B_PARTS = 4
TILE_M = 256
TILE_N = 256


def kernel(a_ref, b_ref, c_ref, a_own, a_far, b_buf, total, own_sem, bown_sem, bsend_sem, brecv_sem, asend_sem, arecv_sem):
    layer, col, row = lax.axis_index("depth"), lax.axis_index("col"), lax.axis_index("row")
    rows = c_ref.shape[0]
    depth, cols = b_ref.shape
    across = (layer, 1 - col, row)
    beside = (layer, col, 1 - row)
    base = layer * rows
    slot = lax.rem(row + col, 2)

    own_a = pltpu.make_async_copy(a_ref.at[pl.ds(base, rows), :], a_own, own_sem)
    own_b = pltpu.make_async_copy(b_ref, b_buf.at[slot], bown_sem)
    own_a.start()
    own_b.start()

    barrier = pltpu.get_barrier_semaphore()
    for peer in (across, beside):
        pl.semaphore_signal(barrier, inc=1, device_id=peer, device_id_type=MESH)
    pl.semaphore_wait(barrier, 2)

    a_sends = []
    start = 0
    for idx, size in enumerate(CHUNKS):
        a_sends.append(
            pltpu.make_async_remote_copy(
                src_ref=a_ref.at[pl.ds(base + start, size), :],
                dst_ref=a_far.at[pl.ds(start, size), :],
                send_sem=asend_sem.at[idx],
                recv_sem=arecv_sem.at[idx],
                device_id=across,
                device_id_type=MESH,
            )
        )
        start += size
    b_sends = []
    part = depth // B_PARTS
    for idx in range(B_PARTS):
        b_sends.append(
            pltpu.make_async_remote_copy(
                src_ref=b_ref.at[pl.ds(idx * part, part), :],
                dst_ref=b_buf.at[slot, pl.ds(idx * part, part), :],
                send_sem=bsend_sem.at[idx],
                recv_sem=brecv_sem.at[idx],
                device_id=beside,
                device_id_type=MESH,
            )
        )
    a_sends[0].start()
    for send in b_sends:
        send.start()
    for send in a_sends[1:]:
        send.start()

    own_a.wait()
    own_b.wait()
    for send in b_sends:
        send.wait_recv()

    col_tiles = cols // TILE_N

    @pl.loop(0, (rows // TILE_M) * col_tiles)
    def _(tile):
        r = pl.ds(pl.multiple_of((tile // col_tiles) * TILE_M, TILE_M), TILE_M)
        c = pl.ds(pl.multiple_of((tile % col_tiles) * TILE_N, TILE_N), TILE_N)
        total[r, c] = jnp.dot(a_own[r, :], b_buf[0, :, c], preferred_element_type=jnp.float32)

    start = 0
    for idx, size in enumerate(CHUNKS):
        a_sends[idx].wait_recv()
        r = pl.ds(start, size)

        @pl.loop(0, col_tiles)
        def _(tile):
            c = pl.ds(pl.multiple_of(tile * TILE_N, TILE_N), TILE_N)
            rest = jnp.dot(a_far[r, :], b_buf[1, :, c], preferred_element_type=jnp.float32)
            c_ref[r, c] = (total[r, c] + rest).astype(c_ref.dtype)

        start += size

    for send in a_sends + b_sends:
        send.wait_send()


def solution(mesh):
    depth_n = mesh.shape["depth"]

    def local_mm(a_blk, b_blk):
        rows = a_blk.shape[0] // depth_n
        depth, cols = b_blk.shape
        n = len(CHUNKS)
        dma = pltpu.SemaphoreType.DMA
        return pl.pallas_call(
            kernel,
            out_shape=jax.ShapeDtypeStruct((rows, cols), jnp.bfloat16),
            in_specs=[pl.BlockSpec(memory_space=pl.ANY)] * 2,
            out_specs=pl.BlockSpec(memory_space=pltpu.VMEM),
            scratch_shapes=[
                pltpu.VMEM((rows, depth), jnp.bfloat16),
                pltpu.VMEM((rows, depth), jnp.bfloat16),
                pltpu.VMEM((2, depth, cols), jnp.bfloat16),
                pltpu.VMEM((rows, cols), jnp.float32),
                dma,
                dma,
                dma((B_PARTS,)),
                dma((B_PARTS,)),
                dma((n,)),
                dma((n,)),
            ],
            compiler_params=pltpu.CompilerParams(
                collective_id=0, has_side_effects=True, vmem_limit_bytes=56 * 1024 * 1024
            ),
            cost_estimate=pl.CostEstimate(flops=4 * rows * depth * cols, bytes_accessed=2 * (6 * depth * cols), transcendentals=0),
        )(a_blk, b_blk)

    return jax.shard_map(
        local_mm, mesh=mesh, in_specs=(P("row", "col"), P("row", "col")), out_specs=P(("row", "depth"), "col"), check_vma=False
    )
```

time: 325 us -> 104 us (0.32)
  waiting for transfers between devices: 275 us -> 0 us
  Pallas kernels: 0 us -> 98.4 us
  matrix products: 20.5 us -> 0 us
  between operations: 13.4 us -> 0.01 us
  starting transfers between devices: 7.97 us -> 0 us
  other arithmetic: 6.05 us -> 0 us
  local copies, waits for them, and re-layouts: 0 us -> 4.79 us
    reduce_scatter x1 -> x0, waiting for transfers between devices: 189 us -> none  [local_mm(): lax.psum_scatter(part_sum, 'depth', scatter_dimension=0, tiled=True)]
    pallas_call x0 -> x1, Pallas kernels: none -> 98.4 us  [local_mm(): pl.pallas_call(kernel, out_shape=jax.ShapeDtypeStruct((rows, cols), jnp.b...]
    ppermute x2 -> x0, waiting for transfers between devices: 86.8 us -> none  [the longest x1 86.8 us: local_mm(): a_first = lax.ppermute(a_blk, AXES_ALL, pairs_a0)]
    dot_general x1 -> x0, matrix products: 20.5 us -> none  [local_mm(): block_prod = jnp.dot(a_cur, b_cur, preferred_element_type=jnp.float32)]
    ppermute x2 -> x0, starting transfers between devices: 7.97 us -> none  [the longest x1 4.04 us: local_mm(): b_cur = lax.ppermute(b_blk, AXES_ALL, pairs_b)]
    convert_element_type x1 -> x0, other arithmetic: 6.05 us -> none  [local_mm(): return c_rows.astype(jnp.bfloat16)]
    unnamed x0 -> x1, local copies, waits for them, and re-layouts: none -> 4.79 us
  transfers between devices with their start and end apart: 3 -> 0, of which waited for: 2 -> 0; matrix products, arithmetic and copies ran while one was open for 0% -> 0% of each run, Pallas kernels for 0% -> 0%
where the time goes in v1:
time: 104 us; the launch traced here: 103 us
  Pallas kernels  98.4 us (95%)
  local copies, waits for them, and re-layouts  4.79 us (5%)
    pallas_call x1, Pallas kernels, local_mm(): pl.pallas_call(kernel, out_shape=jax.ShapeDtypeStruct((rows, cols), jnp.b...  98.4 us
    unnamed x1, local copies, waits for them, and re-layouts  4.79 us

profile of v1, /device:TPU:1, one launch (start us, length us, event | category | flops | bytes accessed | tf_op | source)
XLA Modules:
  0.0 103.2 jit_solution(9979105964041916744)
XLA Ops:
  0.0 98.4 %shard_map.28 = bf16[1024,2048]{1,0:T(8,128)(2,1)} custom-call(bf16[2048,2048]{1,0:T(8,128)(2,1)} %a_ref.1, bf16[2048,2048]{1,0:T(8,128)(2,1)} %b_ref.1), custom_call_target="tpu_custom_call" | custom-call | flops 17179869184 | bytes 50331648 | tf_op jit(solution)/shard_map/pallas_call | solution.py:107
  98.4 4.8 %copy.4 = bf16[1024,2048]{1,0:T(8,128)(2,1)} copy(bf16[1024,2048]{1,0:T(8,128)(2,1)} %shard_map.28) | data formatting | bytes 8388608

commit v2 on v1

v2 whole, which is shorter than its diff:
```python
import jax
import jax.numpy as jnp
from jax import lax
from jax.experimental import pallas as pl
from jax.experimental.pallas import tpu as pltpu
from jax.sharding import PartitionSpec as P

MESH = pl.DeviceIdType.MESH
PIECES = (
    (0, 256, 0, 2048, 8, False),
    (256, 256, 0, 2048, 8, False),
    (512, 256, 0, 2048, 8, False),
    (768, 256, 0, 1024, 8, False),
    (768, 256, 1024, 512, 8, False),
    (768, 256, 1536, 256, 4, True),
    (768, 256, 1792, 256, 4, True),
)
B_PARTS = 4
TILE_M = 256
TILE_N = 256


def kernel(a_ref, b_ref, c_ref, a_own, a_far, b_buf, total, own_sem, bown_sem, bsend_sem, brecv_sem, asend_sem, arecv_sem, ready_sem):
    layer, col, row = lax.axis_index("depth"), lax.axis_index("col"), lax.axis_index("row")
    rows = c_ref.shape[0]
    depth, cols = b_ref.shape
    across = (layer, 1 - col, row)
    beside = (layer, col, 1 - row)
    base = layer * rows
    slot = lax.rem(row + col, 2)

    barrier = pltpu.get_barrier_semaphore()
    pl.semaphore_signal(barrier, inc=1, device_id=across, device_id_type=MESH)

    @pl.when(row == 1)
    def _():
        pl.semaphore_signal(barrier, inc=1, device_id=beside, device_id_type=MESH)
        pl.semaphore_wait(barrier, 1)

    @pl.when(row == 0)
    def _():
        pl.semaphore_wait(barrier, 2)
        pl.semaphore_signal(ready_sem, inc=1, device_id=beside, device_id_type=MESH)

    a_sends = []
    for idx, (r0, nr, k0, nk, _, _) in enumerate(PIECES):
        a_sends.append(
            pltpu.make_async_remote_copy(
                src_ref=a_ref.at[pl.ds(base + r0, nr), pl.ds(k0, nk)],
                dst_ref=a_far.at[pl.ds(r0, nr), pl.ds(k0, nk)],
                send_sem=asend_sem.at[idx],
                recv_sem=arecv_sem.at[idx],
                device_id=across,
                device_id_type=MESH,
            )
        )
    b_sends = []
    part = depth // B_PARTS
    for idx in range(B_PARTS):
        b_sends.append(
            pltpu.make_async_remote_copy(
                src_ref=b_ref.at[pl.ds(idx * part, part), :],
                dst_ref=b_buf.at[slot, pl.ds(idx * part, part), :],
                send_sem=bsend_sem.at[idx],
                recv_sem=brecv_sem.at[idx],
                device_id=beside,
                device_id_type=MESH,
            )
        )
    own_a = pltpu.make_async_copy(a_ref.at[pl.ds(base, rows), :], a_own, own_sem)
    own_b = pltpu.make_async_copy(b_ref, b_buf.at[slot], bown_sem)

    a_sends[0].start()

    @pl.when(row == 1)
    def _():
        pl.semaphore_wait(ready_sem, 1)

    for send in b_sends:
        send.start()
    for send in a_sends[1:]:
        send.start()
    own_a.start()
    own_b.start()
    own_a.wait()
    own_b.wait()
    for send in b_sends:
        send.wait_recv()

    col_tiles = cols // TILE_N

    @pl.loop(0, (rows // TILE_M) * col_tiles)
    def _(tile):
        r = pl.ds(pl.multiple_of((tile // col_tiles) * TILE_M, TILE_M), TILE_M)
        c = pl.ds(pl.multiple_of((tile % col_tiles) * TILE_N, TILE_N), TILE_N)
        total[r, c] = jnp.dot(a_own[r, :], b_buf[0, :, c], preferred_element_type=jnp.float32)

    for idx, (r0, nr, k0, nk, tiles, unroll) in enumerate(PIECES):
        a_sends[idx].wait_recv()
        r, k, tn = pl.ds(r0, nr), pl.ds(k0, nk), cols // tiles

        def add(c):
            sums = total[r, c] + jnp.dot(a_far[r, k], b_buf[1, k, c], preferred_element_type=jnp.float32)
            if k0 + nk == depth:
                c_ref[r, c] = sums.astype(c_ref.dtype)
            else:
                total[r, c] = sums

        if unroll:
            for tile in range(tiles):
                add(pl.ds(tile * tn, tn))
        else:

            @pl.loop(0, tiles)
            def _(tile):
                add(pl.ds(pl.multiple_of(tile * tn, tn), tn))

    for send in a_sends + b_sends:
        send.wait_send()


def solution(mesh):
    depth_n = mesh.shape["depth"]

    def local_mm(a_blk, b_blk):
        rows = a_blk.shape[0] // depth_n
        depth, cols = b_blk.shape
        n = len(PIECES)
        dma = pltpu.SemaphoreType.DMA
        return pl.pallas_call(
            kernel,
            out_shape=pltpu.VMEM((rows, cols), jnp.bfloat16),
            in_specs=[pl.BlockSpec(memory_space=pl.ANY)] * 2,
            out_specs=pl.BlockSpec(memory_space=pltpu.VMEM),
            scratch_shapes=[
                pltpu.VMEM((rows, depth), jnp.bfloat16),
                pltpu.VMEM((rows, depth), jnp.bfloat16),
                pltpu.VMEM((2, depth, cols), jnp.bfloat16),
                pltpu.VMEM((rows, cols), jnp.float32),
                dma,
                dma,
                dma((B_PARTS,)),
                dma((B_PARTS,)),
                dma((n,)),
                dma((n,)),
                pltpu.SemaphoreType.REGULAR,
            ],
            compiler_params=pltpu.CompilerParams(
                collective_id=0, has_side_effects=True, vmem_limit_bytes=56 * 1024 * 1024
            ),
            cost_estimate=pl.CostEstimate(flops=4 * rows * depth * cols, bytes_accessed=12 * depth * cols, transcendentals=0),
        )(a_blk, b_blk)

    return jax.shard_map(
        local_mm, mesh=mesh, in_specs=(P("row", "col"), P("row", "col")), out_specs=P(("row", "depth"), "col"), check_vma=False
    )
```

time: 104 us -> 96.7 us (0.930)
  Pallas kernels: 98.4 us -> 93 us
  local copies, waits for them, and re-layouts: 4.79 us -> 2.02 us
    pallas_call x1, Pallas kernels: 98.4 us -> 93 us  [local_mm(): pl.pallas_call(kernel, out_shape=pltpu.VMEM((rows, cols), jnp.bfloat16),...]
    unnamed x1, local copies, waits for them, and re-layouts: 4.79 us -> 2.02 us
where the time goes in v2:
time: 96.7 us; the launch traced here: 95 us
  Pallas kernels  93 us (96%)
  local copies, waits for them, and re-layouts  2.02 us (2%)
    pallas_call x1, Pallas kernels, local_mm(): pl.pallas_call(kernel, out_shape=pltpu.VMEM((rows, cols), jnp.bfloat16),...  93 us
    unnamed x1, local copies, waits for them, and re-layouts  2.02 us

profile of v2, /device:TPU:1, one launch (start us, length us, event | category | flops | bytes accessed | tf_op | source)
XLA Modules:
  0.0 95.0 jit_solution(15793965011967880168)
XLA Ops:
  0.0 93.0 %shard_map.28 = bf16[1024,2048]{1,0:T(8,128)(2,1)S(1)} custom-call(bf16[2048,2048]{1,0:T(8,128)(2,1)} %a_ref.1, bf16[2048,2048]{1,0:T(8,128)(2,1)} %b_ref.1), custom_call_target="tpu_custom_call" | custom-call | flops 17179869184 | bytes 50331648 | tf_op jit(solution)/shard_map/pallas_call | solution.py:130
  93.0 2.0 %copy.4 = bf16[1024,2048]{1,0:T(8,128)(2,1)} copy(bf16[1024,2048]{1,0:T(8,128)(2,1)S(1)} %shard_map.28) | data formatting | bytes 8388608

commit v3 on v2

v3 whole, which is shorter than its diff:
```python
import functools

import jax
import jax.numpy as jnp
from jax import lax
from jax.experimental import pallas as pl
from jax.experimental.pallas import tpu as pltpu
from jax.sharding import PartitionSpec as P

MESH = pl.DeviceIdType.MESH
BOTTOM = 192
FIRST = (
    (0, 256, 0, 2048),
    (256, 256, 0, 2048),
    (512, 128, 0, 2048),
    (640, 64, 0, 2048),
    (704, 128, 0, 512),
    (704, 128, 512, 512),
    (704, 128, 1024, 512),
    (704, 128, 1536, 512),
)
SECOND = (
    (0, 192, 0, 1024),
    (0, 192, 1024, 512),
    (0, 192, 1536, 256),
    (0, 192, 1792, 256),
)
HOLD = 3
TURN = 4
B_PARTS = 4
TILE_M = 256
TILE_N = 256


def place():
    layer, col, row = lax.axis_index("depth"), lax.axis_index("col"), lax.axis_index("row")
    return layer, row, (layer, 1 - col, row), (layer, col, 1 - row), lax.rem(row + col, 2)


def sends_of(pieces, a_ref, first_row, a_far, send_sem, recv_sem, device):
    return [
        pltpu.make_async_remote_copy(
            src_ref=a_ref.at[pl.ds(first_row + r0, nr), pl.ds(k0, nk)],
            dst_ref=a_far.at[pl.ds(r0, nr), pl.ds(k0, nk)],
            send_sem=send_sem.at[idx],
            recv_sem=recv_sem.at[idx],
            device_id=device,
            device_id_type=MESH,
        )
        for idx, (r0, nr, k0, nk) in enumerate(pieces)
    ]


def multiply(piece, a_far, b_far, total, c_ref):
    r0, nr, k0, nk = piece
    depth, cols = b_far.shape
    r, k = pl.ds(r0, nr), pl.ds(k0, nk)

    def add(c):
        sums = total[r, c] + jnp.dot(a_far[r, k], b_far[k, c], preferred_element_type=jnp.float32)
        if k0 + nk == depth:
            c_ref[r, c] = sums.astype(c_ref.dtype)
        else:
            total[r, c] = sums

    if nk <= 512:
        for tile in range(4):
            add(pl.ds(tile * (cols // 4), cols // 4))
    else:

        @pl.loop(0, cols // TILE_N)
        def _(tile):
            add(pl.ds(pl.multiple_of(tile * TILE_N, TILE_N), TILE_N))


def first_kernel(
    a_ref, b_ref, c_ref, b_far, low, a_own, a_far, b_near, total, own_sem, bown_sem, bsend_sem, brecv_sem, asend_sem, arecv_sem, ready_sem, turn_sem
):
    layer, row, across, beside, slot = place()
    top, cols = c_ref.shape
    rows, depth = a_own.shape
    base = layer * rows

    barrier = pltpu.get_barrier_semaphore()
    pl.semaphore_signal(barrier, inc=1, device_id=across, device_id_type=MESH)

    @pl.when(row == 1)
    def _():
        pl.semaphore_signal(barrier, inc=1, device_id=beside, device_id_type=MESH)
        pl.semaphore_wait(barrier, 1)

    @pl.when(row == 0)
    def _():
        pl.semaphore_wait(barrier, 2)
        pl.semaphore_signal(ready_sem, inc=1, device_id=beside, device_id_type=MESH)

    a_sends = sends_of(FIRST, a_ref, base, a_far, asend_sem, arecv_sem, across)
    part = depth // B_PARTS

    def sends_of_b(b_buf):
        return [
            pltpu.make_async_remote_copy(
                src_ref=b_ref.at[pl.ds(idx * part, part), :],
                dst_ref=b_buf.at[pl.ds(idx * part, part), :],
                send_sem=bsend_sem.at[idx],
                recv_sem=brecv_sem.at[idx],
                device_id=beside,
                device_id_type=MESH,
            )
            for idx in range(B_PARTS)
        ]

    def own_of_b(b_buf):
        return pltpu.make_async_copy(b_ref, b_buf, bown_sem)

    own_a = pltpu.make_async_copy(a_ref.at[pl.ds(base, rows), :], a_own, own_sem)

    a_sends[0].start()

    @pl.when(row == 1)
    def _():
        pl.semaphore_wait(ready_sem, 1)

    for value, b_buf in enumerate((b_near, b_far)):

        @pl.when(slot == value)
        def _():
            for send in sends_of_b(b_buf):
                send.start()

    for send in a_sends[1:HOLD]:
        send.start()

    @pl.when(row == 0)
    def _():
        for send in a_sends[HOLD:]:
            send.start()

    own_a.start()
    for value, b_buf in enumerate((b_near, b_far)):

        @pl.when(slot == value)
        def _():
            own_of_b(b_buf).start()

    own_a.wait()
    for value, (b_mine, b_other) in enumerate(((b_near, b_far), (b_far, b_near))):

        @pl.when(slot == value)
        def _():
            own_of_b(b_mine).wait()
            for send in sends_of_b(b_other):
                send.wait_recv()


    col_tiles = cols // TILE_N

    tile_m = top // 4

    @pl.loop(0, 4 * col_tiles)
    def _(tile):
        r = pl.ds(pl.multiple_of((tile // col_tiles) * tile_m, 16), tile_m)
        c = pl.ds(pl.multiple_of((tile % col_tiles) * TILE_N, TILE_N), TILE_N)
        total[r, c] = jnp.dot(a_own[r, :], b_near[:, c], preferred_element_type=jnp.float32)

    @pl.loop(0, col_tiles)
    def _(tile):
        c = pl.ds(pl.multiple_of(tile * TILE_N, TILE_N), TILE_N)
        low[:, c] = jnp.dot(a_own[pl.ds(top, rows - top), :], b_near[:, c], preferred_element_type=jnp.float32)

    for idx, piece in enumerate(FIRST):
        if idx == HOLD:

            @pl.when(row == 1)
            def _():
                pl.semaphore_wait(turn_sem, 1)
                for send in a_sends[HOLD:]:
                    send.start()

        a_sends[idx].wait_recv()
        if idx == TURN:

            @pl.when(row == 0)
            def _():
                a_sends[TURN].wait_send()
                pl.semaphore_signal(turn_sem, inc=1, device_id=beside, device_id_type=MESH)

        multiply(piece, a_far, b_far, total, c_ref)

    for idx, send in enumerate(a_sends):
        if idx != TURN:
            send.wait_send()

    @pl.when(row == 1)
    def _():
        a_sends[TURN].wait_send()

    for value, b_buf in enumerate((b_near, b_far)):

        @pl.when(slot == value)
        def _():
            for send in sends_of_b(b_buf):
                send.wait_send()


def second_kernel(a_ref, token_ref, b_far, low_ref, c_ref, a_far, total, asend_sem, arecv_sem):
    del token_ref
    layer, _, across, _, _ = place()
    bottom, cols = c_ref.shape
    rows = a_ref.shape[0] // 2

    barrier = pltpu.get_barrier_semaphore()
    pl.semaphore_signal(barrier, inc=1, device_id=across, device_id_type=MESH)
    pl.semaphore_wait(barrier, 1)
    a_sends = sends_of(SECOND, a_ref, layer * rows + rows - bottom, a_far, asend_sem, arecv_sem, across)
    for send in a_sends:
        send.start()
    total[...] = low_ref[...]
    for idx, piece in enumerate(SECOND):
        a_sends[idx].wait_recv()
        multiply(piece, a_far, b_far, total, c_ref)
    for send in a_sends:
        send.wait_send()


def write_top(top_ref, out_ref, token_ref, sem):
    copy = pltpu.make_async_copy(top_ref, out_ref.at[pl.ds(0, top_ref.shape[0]), :], sem)
    copy.start()
    token_ref[...] = jnp.zeros_like(token_ref)
    copy.wait()


def write_bottom(half_ref, low_ref, out_ref, sem):
    del half_ref
    rows, bottom = out_ref.shape[0], low_ref.shape[0]
    copy = pltpu.make_async_copy(low_ref, out_ref.at[pl.ds(rows - bottom, bottom), :], sem)
    copy.start()
    copy.wait()


def solution(mesh):
    depth_n = mesh.shape["depth"]
    dma = pltpu.SemaphoreType.DMA
    hbm, vmem = pl.BlockSpec(memory_space=pltpu.HBM), pl.BlockSpec(memory_space=pltpu.VMEM)

    def local_mm(a_blk, b_blk):
        rows = a_blk.shape[0] // depth_n
        depth, cols = b_blk.shape
        c_type = jax.ShapeDtypeStruct((rows, cols), jnp.bfloat16)
        params = functools.partial(pltpu.CompilerParams, has_side_effects=True)
        c_top, b_far, low = pl.pallas_call(
            first_kernel,
            out_shape=(
                pltpu.VMEM((rows - BOTTOM, cols), jnp.bfloat16),
                pltpu.VMEM((depth, cols), jnp.bfloat16),
                pltpu.VMEM((BOTTOM, cols), jnp.float32),
            ),
            in_specs=[hbm, hbm],
            out_specs=(vmem, vmem, vmem),
            scratch_shapes=[
                pltpu.VMEM((rows, depth), jnp.bfloat16),
                pltpu.VMEM((rows - BOTTOM, depth), jnp.bfloat16),
                pltpu.VMEM((depth, cols), jnp.bfloat16),
                pltpu.VMEM((rows - BOTTOM, cols), jnp.float32),
                dma,
                dma,
                dma((B_PARTS,)),
                dma((B_PARTS,)),
                dma((len(FIRST),)),
                dma((len(FIRST),)),
                pltpu.SemaphoreType.REGULAR,
                pltpu.SemaphoreType.REGULAR,
            ],
            compiler_params=params(collective_id=0, vmem_limit_bytes=40 * 1024 * 1024),
            cost_estimate=pl.CostEstimate(flops=4 * rows * depth * cols, bytes_accessed=12 * depth * cols, transcendentals=0),
        )(a_blk, b_blk)
        written, token = pl.pallas_call(
            write_top,
            out_shape=(c_type, pltpu.VMEM((8, 128), jnp.float32)),
            in_specs=[vmem],
            out_specs=(hbm, vmem),
            scratch_shapes=[dma],
            compiler_params=pltpu.CompilerParams(vmem_limit_bytes=16 * 1024 * 1024),
        )(c_top)
        c_low = pl.pallas_call(
            second_kernel,
            out_shape=pltpu.VMEM((BOTTOM, cols), jnp.bfloat16),
            in_specs=[hbm, vmem, vmem, vmem],
            out_specs=vmem,
            scratch_shapes=[
                pltpu.VMEM((BOTTOM, depth), jnp.bfloat16),
                pltpu.VMEM((BOTTOM, cols), jnp.float32),
                dma((len(SECOND),)),
                dma((len(SECOND),)),
            ],
            compiler_params=params(collective_id=1, vmem_limit_bytes=16 * 1024 * 1024),
        )(a_blk, token, b_far, low)
        return pl.pallas_call(
            write_bottom,
            out_shape=c_type,
            in_specs=[hbm, vmem],
            out_specs=hbm,
            scratch_shapes=[dma],
            input_output_aliases={0: 0},
            compiler_params=pltpu.CompilerParams(vmem_limit_bytes=16 * 1024 * 1024),
        )(written, c_low)

    return jax.shard_map(
        local_mm, mesh=mesh, in_specs=(P("row", "col"), P("row", "col")), out_specs=P(("row", "depth"), "col"), check_vma=False
    )
```

time: 96.7 us -> 94.4 us (0.976); the launches traced: 95 us -> 94.3 us
  local copies, waits for them, and re-layouts: 2.02 us -> 0.01 us
  Pallas kernels: 93 us -> 94.3 us
    unnamed x1 -> x2, local copies, waits for them, and re-layouts: 2.02 us -> 0.01 us
    pallas_call x1 -> x4, Pallas kernels: 93 us -> 94.3 us  [the longest x1 78.4 us: local_mm(): pl.pallas_call(first_kernel, out_shape=(pltpu.VMEM((rows - BOTTOM, cols),...]
where the time goes in v3:
time: 94.4 us; the launch traced here: 94.3 us
  Pallas kernels  94.3 us (100%)
    pallas_call x1, Pallas kernels, local_mm(): pl.pallas_call(first_kernel, out_shape=(pltpu.VMEM((rows - BOTTOM, cols),...  78.4 us
    pallas_call x1, Pallas kernels, local_mm(): pl.pallas_call(second_kernel, out_shape=pltpu.VMEM((BOTTOM, cols), jnp.bf...  13.2 us

profile of v3, /device:TPU:1, one launch (start us, length us, event | category | flops | bytes accessed | tf_op | source)
XLA Modules:
  0.0 94.3 jit_solution(14507749576631029342)
XLA Ops:
  0.0 0.0 copy-start
  0.0 78.4 %shard_map.28 = (bf16[832,2048]{1,0:T(8,128)(2,1)S(1)}, bf16[2048,2048]{1,0:T(8,128)(2,1)S(1)}, f32[192,2048]{1,0:T(8,128)S(1)}) custom-call(bf16[2048,2048]{1,0:T(8,128)(2,1)} %a_ref.3, bf16[2048,2048]{1,0:T(8,128)(2,1)} %b_ref.1), custom_call_target="tpu_custom_call" | custom-call | flops 17179869184 | bytes 50331648 | tf_op jit(solution)/shard_map/pallas_call | solution.py:251
  78.4 1.8 %shard_map.29 = (bf16[1024,2048]{1,0:T(8,128)(2,1)}, f32[8,128]{1,0:T(8,128)S(1)}) custom-call(bf16[832,2048]{1,0:T(8,128)(2,1)S(1)} %get-tuple-element.10.top_ref), custom_call_target="tpu_custom_call" | custom-call | tf_op jit(solution)/shard_map/pallas_call | solution.py:277
  80.2 0.0 copy-done
  80.2 13.2 %shard_map.30.low_ref = bf16[192,2048]{1,0:T(8,128)(2,1)S(1)} custom-call(bf16[2048,2048]{1,0:T(8,128)(2,1)S(1)} %copy-done, f32[8,128]{1,0:T(8,128)S(1)} %get-tuple-element.12.token_ref, bf16[2048,2048]{1,0:T(8,128)(2,1)S(1)} %get-tuple-element.13.b_far, f32[192,2048]{1,0:T(8,128)S(1)} %get-tuple-element.14.low_ref), custom_call_target="tpu_custom_call" | custom-call | tf_op jit(solution)/shard_map/pallas_call | solution.py:285
  93.4 0.9 shard_map.31
Async XLA Ops:
  0.0 80.2 %copy-start = (bf16[2048,2048]{1,0:T(8,128)(2,1)S(1)}, bf16[2048,2048]{1,0:T(8,128)(2,1)}, u32[]{:S(2)}) copy-start(bf16[2048,2048]{1,0:T(8,128)(2,1)} %a_ref.3) | copy-start | bytes 25165828

commit v4 on v3

--- a/solution.py
+++ b/solution.py
@@ -12,7 +12,8 @@
 FIRST = (
     (0, 256, 0, 2048),
     (256, 256, 0, 2048),
-    (512, 128, 0, 2048),
+    (632, 8, 0, 2048),
+    (512, 120, 0, 2048),
     (640, 64, 0, 2048),
     (704, 128, 0, 512),
     (704, 128, 512, 512),
@@ -23,18 +24,19 @@
     (0, 192, 0, 1024),
     (0, 192, 1024, 512),
     (0, 192, 1536, 256),
-    (0, 192, 1792, 256),
+    (0, 128, 1792, 256),
+    (128, 64, 1792, 256),
 )
-HOLD = 3
-TURN = 4
+AROUND = 2
+HOLD = 4
+TURN = 5
 B_PARTS = 4
-TILE_M = 256
 TILE_N = 256
 
 
 def place():
     layer, col, row = lax.axis_index("depth"), lax.axis_index("col"), lax.axis_index("row")
-    return layer, row, (layer, 1 - col, row), (layer, col, 1 - row), lax.rem(row + col, 2)
+    return layer, col, row, (layer, 1 - col, row), (layer, col, 1 - row), lax.rem(row + col, 2)
 
 
 def sends_of(pieces, a_ref, first_row, a_far, send_sem, recv_sem, device):
@@ -74,9 +76,27 @@
 
 
 def first_kernel(
-    a_ref, b_ref, c_ref, b_far, low, a_own, a_far, b_near, total, own_sem, bown_sem, bsend_sem, brecv_sem, asend_sem, arecv_sem, ready_sem, turn_sem
+    a_ref,
+    b_ref,
+    c_ref,
+    b_far,
+    low,
+    a_own,
+    a_far,
+    b_near,
+    total,
+    own_sem,
+    bown_sem,
+    bsend_sem,
+    brecv_sem,
+    asend_sem,
+    arecv_sem,
+    ready_sem,
+    turn_sem,
+    passing,
+    pass_sem,
 ):
-    layer, row, across, beside, slot = place()
+    layer, col, row, across, beside, slot = place()
     top, cols = c_ref.shape
     rows, depth = a_own.shape
     base = layer * rows
@@ -84,9 +104,24 @@
     barrier = pltpu.get_barrier_semaphore()
     pl.semaphore_signal(barrier, inc=1, device_id=across, device_id_type=MESH)
 
+    upper = jnp.logical_and(row == 1, layer == 0)
+    lower = jnp.logical_and(row == 1, layer == 1)
+    below = (1 - layer, col, row)
+
     @pl.when(row == 1)
     def _():
         pl.semaphore_signal(barrier, inc=1, device_id=beside, device_id_type=MESH)
+
+    @pl.when(upper)
+    def _():
+        pl.semaphore_signal(barrier, inc=1, device_id=below, device_id_type=MESH)
+
+    @pl.when(lower)
+    def _():
+        pl.semaphore_wait(barrier, 2)
+
+    @pl.when(upper)
+    def _():
         pl.semaphore_wait(barrier, 1)
 
     @pl.when(row == 0)
@@ -95,6 +130,23 @@
         pl.semaphore_signal(ready_sem, inc=1, device_id=beside, device_id_type=MESH)
 
     a_sends = sends_of(FIRST, a_ref, base, a_far, asend_sem, arecv_sem, across)
+    r0, nr, k0, nk = FIRST[AROUND]
+    to_relay = pltpu.make_async_remote_copy(
+        src_ref=a_ref.at[pl.ds(r0, nr), pl.ds(k0, nk)],
+        dst_ref=passing,
+        send_sem=pass_sem.at[0],
+        recv_sem=pass_sem.at[1],
+        device_id=across,
+        device_id_type=MESH,
+    )
+    from_relay = pltpu.make_async_remote_copy(
+        src_ref=passing,
+        dst_ref=a_far.at[pl.ds(r0, nr), pl.ds(k0, nk)],
+        send_sem=pass_sem.at[2],
+        recv_sem=arecv_sem.at[AROUND],
+        device_id=below,
+        device_id_type=MESH,
+    )
     part = depth // B_PARTS
 
     def sends_of_b(b_buf):
@@ -128,7 +180,17 @@
             for send in sends_of_b(b_buf):
                 send.start()
 
-    for send in a_sends[1:HOLD]:
+    @pl.when(lower)
+    def _():
+        to_relay.start()
+
+    a_sends[1].start()
+
+    @pl.when(jnp.logical_not(upper))
+    def _():
+        a_sends[AROUND].start()
+
+    for send in a_sends[AROUND + 1 : HOLD]:
         send.start()
 
     @pl.when(row == 0)
@@ -152,9 +214,7 @@
             for send in sends_of_b(b_other):
                 send.wait_recv()
 
-
     col_tiles = cols // TILE_N
-
     tile_m = top // 4
 
     @pl.loop(0, 4 * col_tiles)
@@ -185,11 +245,29 @@
                 a_sends[TURN].wait_send()
                 pl.semaphore_signal(turn_sem, inc=1, device_id=beside, device_id_type=MESH)
 
-        multiply(piece, a_far, b_far, total, c_ref)
+        if idx == AROUND + 1:
+            piece = (piece[0], piece[1] + FIRST[AROUND][1], *piece[2:])
+        if idx != AROUND:
+            multiply(piece, a_far, b_far, total, c_ref)
+        if idx == 0:
+
+            @pl.when(lower)
+            def _():
+                to_relay.wait_recv()
+                from_relay.start()
 
     for idx, send in enumerate(a_sends):
-        if idx != TURN:
+        if idx not in (TURN, AROUND):
             send.wait_send()
+
+    @pl.when(jnp.logical_not(upper))
+    def _():
+        a_sends[AROUND].wait_send()
+
+    @pl.when(lower)
+    def _():
+        to_relay.wait_send()
+        from_relay.wait_send()
 
     @pl.when(row == 1)
     def _():
@@ -205,9 +283,8 @@
 
 def second_kernel(a_ref, token_ref, b_far, low_ref, c_ref, a_far, total, asend_sem, arecv_sem):
     del token_ref
-    layer, _, across, _, _ = place()
-    bottom, cols = c_ref.shape
-    rows = a_ref.shape[0] // 2
+    layer, _, _, across, _, _ = place()
+    bottom, rows = total.shape[0], a_ref.shape[0] // 2
 
     barrier = pltpu.get_barrier_semaphore()
     pl.semaphore_signal(barrier, inc=1, device_id=across, device_id_type=MESH)
@@ -218,7 +295,8 @@
     total[...] = low_ref[...]
     for idx, piece in enumerate(SECOND):
         a_sends[idx].wait_recv()
-        multiply(piece, a_far, b_far, total, c_ref)
+        if idx + 1 < len(SECOND):
+            multiply(piece, a_far, b_far, total, c_ref)
     for send in a_sends:
         send.wait_send()
 
@@ -230,12 +308,22 @@
     copy.wait()
 
 
-def write_bottom(half_ref, low_ref, out_ref, sem):
+def write_bottom(half_ref, ready_ref, a_far, total, b_far, out_ref, last, ready_sem, last_sem):
     del half_ref
-    rows, bottom = out_ref.shape[0], low_ref.shape[0]
-    copy = pltpu.make_async_copy(low_ref, out_ref.at[pl.ds(rows - bottom, bottom), :], sem)
-    copy.start()
-    copy.wait()
+    rows, ready = out_ref.shape[0], ready_ref.shape[0]
+    r0, nr, k0, nk = SECOND[-1]
+    first_row = rows - r0 - nr
+    ready_copy = pltpu.make_async_copy(ready_ref, out_ref.at[pl.ds(first_row, ready), :], ready_sem)
+    ready_copy.start()
+    tn = last.shape[1] // 4
+    for tile in range(4):
+        r, k, c = pl.ds(r0, nr), pl.ds(k0, nk), pl.ds(tile * tn, tn)
+        sums = total[r, c] + jnp.dot(a_far[r, k], b_far[k, c], preferred_element_type=jnp.float32)
+        last[:, c] = sums.astype(last.dtype)
+    last_copy = pltpu.make_async_copy(last, out_ref.at[pl.ds(first_row + r0, nr), :], last_sem)
+    last_copy.start()
+    ready_copy.wait()
+    last_copy.wait()
 
 
 def solution(mesh):
@@ -270,6 +358,8 @@
                 dma((len(FIRST),)),
                 pltpu.SemaphoreType.REGULAR,
                 pltpu.SemaphoreType.REGULAR,
+                pltpu.VMEM(FIRST[AROUND][1::2], jnp.bfloat16),
+                dma((3,)),
             ],
             compiler_params=params(collective_id=0, vmem_limit_bytes=40 * 1024 * 1024),
             cost_estimate=pl.CostEstimate(flops=4 * rows * depth * cols, bytes_accessed=12 * depth * cols, transcendentals=0),
@@ -282,14 +372,16 @@
             scratch_shapes=[dma],
             compiler_params=pltpu.CompilerParams(vmem_limit_bytes=16 * 1024 * 1024),
         )(c_top)
-        c_low = pl.pallas_call(
+        c_ready, a_far, low_total = pl.pallas_call(
             second_kernel,
-            out_shape=pltpu.VMEM((BOTTOM, cols), jnp.bfloat16),
-            in_specs=[hbm, vmem, vmem, vmem],
-            out_specs=vmem,
-            scratch_shapes=[
+            out_shape=(
+                pltpu.VMEM((SECOND[-1][0], cols), jnp.bfloat16),
                 pltpu.VMEM((BOTTOM, depth), jnp.bfloat16),
                 pltpu.VMEM((BOTTOM, cols), jnp.float32),
+            ),
+            in_specs=[hbm, vmem, vmem, vmem],
+            out_specs=(vmem, vmem, vmem),
+            scratch_shapes=[
                 dma((len(SECOND),)),
                 dma((len(SECOND),)),
             ],
@@ -298,12 +390,12 @@
         return pl.pallas_call(
             write_bottom,
             out_shape=c_type,
-            in_specs=[hbm, vmem],
+            in_specs=[hbm, vmem, vmem, vmem, vmem],
             out_specs=hbm,
-            scratch_shapes=[dma],
+            scratch_shapes=[pltpu.VMEM((SECOND[-1][1], cols), jnp.bfloat16), dma, dma],
             input_output_aliases={0: 0},
             compiler_params=pltpu.CompilerParams(vmem_limit_bytes=16 * 1024 * 1024),
-        )(written, c_low)
+        )(written, c_ready, a_far, low_total, b_far)
 
     return jax.shard_map(
         local_mm, mesh=mesh, in_specs=(P("row", "col"), P("row", "col")), out_specs=P(("row", "depth"), "col"), check_vma=False

time: 94.4 us -> 93.9 us (level)
  no operation moved by 1% of the time
where the time goes in v4:
time: 93.9 us; the launch traced here: 93.7 us
  Pallas kernels  93.7 us (100%)
    pallas_call x1, Pallas kernels, local_mm(): pl.pallas_call(first_kernel, out_shape=(pltpu.VMEM((rows - BOTTOM, cols),...  78 us
    pallas_call x1, Pallas kernels, local_mm(): pl.pallas_call(second_kernel, out_shape=(pltpu.VMEM((SECOND[-1][0], cols)...  12.9 us

profile of v4, /device:TPU:1, one launch (start us, length us, event | category | flops | bytes accessed | tf_op | source)
XLA Modules:
  0.0 93.7 jit_solution(5506937785326947491)
XLA Ops:
  0.0 0.0 copy-start
  0.0 78.0 %shard_map.28 = (bf16[832,2048]{1,0:T(8,128)(2,1)S(1)}, bf16[2048,2048]{1,0:T(8,128)(2,1)S(1)}, f32[192,2048]{1,0:T(8,128)S(1)}) custom-call(bf16[2048,2048]{1,0:T(8,128)(2,1)} %a_ref.3, bf16[2048,2048]{1,0:T(8,128)(2,1)} %b_ref.1), custom_call_target="tpu_custom_call" | custom-call | flops 17179869184 | bytes 50331648 | tf_op jit(solution)/shard_map/pallas_call | solution.py:339
  78.0 1.8 %shard_map.29 = (bf16[1024,2048]{1,0:T(8,128)(2,1)}, f32[8,128]{1,0:T(8,128)S(1)}) custom-call(bf16[832,2048]{1,0:T(8,128)(2,1)S(1)} %get-tuple-element.13.top_ref), custom_call_target="tpu_custom_call" | custom-call | tf_op jit(solution)/shard_map/pallas_call | solution.py:367
  79.8 0.0 copy-done
  79.8 12.9 %shard_map.30 = (bf16[128,2048]{1,0:T(8,128)(2,1)S(1)}, bf16[192,2048]{1,0:T(8,128)(2,1)S(1)}, f32[192,2048]{1,0:T(8,128)S(1)}) custom-call(bf16[2048,2048]{1,0:T(8,128)(2,1)S(1)} %copy-done, f32[8,128]{1,0:T(8,128)S(1)} %get-tuple-element.15.token_ref, bf16[2048,2048]{1,0:T(8,128)(2,1)S(1)} %get-tuple-element.16.b_far, ...), custom_call_target="tpu_custom_call" | custom-call | tf_op jit(solution)/shard_map/pallas_call | solution.py:375
  92.7 1.0 %shard_map.31 = bf16[1024,2048]{1,0:T(8,128)(2,1)} custom-call(bf16[1024,2048]{1,0:T(8,128)(2,1)} %get-tuple-element.14.half_ref, bf16[128,2048]{1,0:T(8,128)(2,1)S(1)} %get-tuple-element.18.ready_ref, bf16[192,2048]{1,0:T(8,128)(2,1)S(1)} %get-tuple-element.19.a_far, f32[192,2048]{1,0:T(8,128)S(1)} %get-tuple-element.20.total, ...), custom_call_target="tpu_custom_call", output_to_operand_aliasing={{}: (0, {})} | custom-call | tf_op jit(solution)/shard_map/pallas_call | solution.py:390
Async XLA Ops:
  0.0 79.8 %copy-start = (bf16[2048,2048]{1,0:T(8,128)(2,1)S(1)}, bf16[2048,2048]{1,0:T(8,128)(2,1)}, u32[]{:S(2)}) copy-start(bf16[2048,2048]{1,0:T(8,128)(2,1)} %a_ref.3) | copy-start | bytes 25165828

commit v5 on v4

--- a/solution.py
+++ b/solution.py
@@ -39,10 +39,10 @@
     return layer, col, row, (layer, 1 - col, row), (layer, col, 1 - row), lax.rem(row + col, 2)
 
 
-def sends_of(pieces, a_ref, first_row, a_far, send_sem, recv_sem, device):
+def sends_of(pieces, a_src, a_far, send_sem, recv_sem, device):
     return [
         pltpu.make_async_remote_copy(
-            src_ref=a_ref.at[pl.ds(first_row + r0, nr), pl.ds(k0, nk)],
+            src_ref=a_src.at[pl.ds(r0, nr), pl.ds(k0, nk)],
             dst_ref=a_far.at[pl.ds(r0, nr), pl.ds(k0, nk)],
             send_sem=send_sem.at[idx],
             recv_sem=recv_sem.at[idx],
@@ -81,11 +81,13 @@
     c_ref,
     b_far,
     low,
+    a_low,
     a_own,
     a_far,
     b_near,
     total,
     own_sem,
+    low_sem,
     bown_sem,
     bsend_sem,
     brecv_sem,
@@ -98,8 +100,8 @@
 ):
     layer, col, row, across, beside, slot = place()
     top, cols = c_ref.shape
-    rows, depth = a_own.shape
-    base = layer * rows
+    bottom, depth = a_low.shape
+    base = layer * (top + bottom)
 
     barrier = pltpu.get_barrier_semaphore()
     pl.semaphore_signal(barrier, inc=1, device_id=across, device_id_type=MESH)
@@ -129,7 +131,9 @@
         pl.semaphore_wait(barrier, 2)
         pl.semaphore_signal(ready_sem, inc=1, device_id=beside, device_id_type=MESH)
 
-    a_sends = sends_of(FIRST, a_ref, base, a_far, asend_sem, arecv_sem, across)
+    a_sends = sends_of(FIRST, a_own, a_far, asend_sem, arecv_sem, across)
+    first_rows = a_ref.at[pl.ds(base, FIRST[0][1]), :]
+    a_sends[0] = sends_of(FIRST[:1], first_rows, a_far, asend_sem, arecv_sem, across)[0]
     r0, nr, k0, nk = FIRST[AROUND]
     to_relay = pltpu.make_async_remote_copy(
         src_ref=a_ref.at[pl.ds(r0, nr), pl.ds(k0, nk)],
@@ -165,9 +169,12 @@
     def own_of_b(b_buf):
         return pltpu.make_async_copy(b_ref, b_buf, bown_sem)
 
-    own_a = pltpu.make_async_copy(a_ref.at[pl.ds(base, rows), :], a_own, own_sem)
+    own_a = pltpu.make_async_copy(a_ref.at[pl.ds(base, top), :], a_own, own_sem)
+    own_low = pltpu.make_async_copy(a_ref.at[pl.ds(base + top, bottom), :], a_low, low_sem)
 
     a_sends[0].start()
+    own_a.start()
+    own_low.start()
 
     @pl.when(row == 1)
     def _():
@@ -184,6 +191,7 @@
     def _():
         to_relay.start()
 
+    own_a.wait()
     a_sends[1].start()
 
     @pl.when(jnp.logical_not(upper))
@@ -198,14 +206,13 @@
         for send in a_sends[HOLD:]:
             send.start()
 
-    own_a.start()
     for value, b_buf in enumerate((b_near, b_far)):
 
         @pl.when(slot == value)
         def _():
             own_of_b(b_buf).start()
 
-    own_a.wait()
+    own_low.wait()
     for value, (b_mine, b_other) in enumerate(((b_near, b_far), (b_far, b_near))):
 
         @pl.when(slot == value)
@@ -226,7 +233,7 @@
     @pl.loop(0, col_tiles)
     def _(tile):
         c = pl.ds(pl.multiple_of(tile * TILE_N, TILE_N), TILE_N)
-        low[:, c] = jnp.dot(a_own[pl.ds(top, rows - top), :], b_near[:, c], preferred_element_type=jnp.float32)
+        low[:, c] = jnp.dot(a_low[...], b_near[:, c], preferred_element_type=jnp.float32)
 
     for idx, piece in enumerate(FIRST):
         if idx == HOLD:
@@ -281,15 +288,14 @@
                 send.wait_send()
 
 
-def second_kernel(a_ref, token_ref, b_far, low_ref, c_ref, a_far, total, asend_sem, arecv_sem):
+def second_kernel(a_low, token_ref, b_far, low_ref, c_ref, a_far, total, asend_sem, arecv_sem):
     del token_ref
-    layer, _, _, across, _, _ = place()
-    bottom, rows = total.shape[0], a_ref.shape[0] // 2
+    _, _, _, across, _, _ = place()
 
     barrier = pltpu.get_barrier_semaphore()
     pl.semaphore_signal(barrier, inc=1, device_id=across, device_id_type=MESH)
     pl.semaphore_wait(barrier, 1)
-    a_sends = sends_of(SECOND, a_ref, layer * rows + rows - bottom, a_far, asend_sem, arecv_sem, across)
+    a_sends = sends_of(SECOND, a_low, a_far, asend_sem, arecv_sem, across)
     for send in a_sends:
         send.start()
     total[...] = low_ref[...]
@@ -316,14 +322,15 @@
     ready_copy = pltpu.make_async_copy(ready_ref, out_ref.at[pl.ds(first_row, ready), :], ready_sem)
     ready_copy.start()
     tn = last.shape[1] // 4
+    copies = [ready_copy]
     for tile in range(4):
         r, k, c = pl.ds(r0, nr), pl.ds(k0, nk), pl.ds(tile * tn, tn)
         sums = total[r, c] + jnp.dot(a_far[r, k], b_far[k, c], preferred_element_type=jnp.float32)
         last[:, c] = sums.astype(last.dtype)
-    last_copy = pltpu.make_async_copy(last, out_ref.at[pl.ds(first_row + r0, nr), :], last_sem)
-    last_copy.start()
-    ready_copy.wait()
-    last_copy.wait()
+        copies.append(pltpu.make_async_copy(last.at[:, c], out_ref.at[pl.ds(first_row + r0, nr), c], last_sem.at[tile]))
+        copies[-1].start()
+    for copy in copies:
+        copy.wait()
 
 
 def solution(mesh):
@@ -336,20 +343,22 @@
         depth, cols = b_blk.shape
         c_type = jax.ShapeDtypeStruct((rows, cols), jnp.bfloat16)
         params = functools.partial(pltpu.CompilerParams, has_side_effects=True)
-        c_top, b_far, low = pl.pallas_call(
+        c_top, b_far, low, a_low = pl.pallas_call(
             first_kernel,
             out_shape=(
                 pltpu.VMEM((rows - BOTTOM, cols), jnp.bfloat16),
                 pltpu.VMEM((depth, cols), jnp.bfloat16),
                 pltpu.VMEM((BOTTOM, cols), jnp.float32),
+                pltpu.VMEM((BOTTOM, depth), jnp.bfloat16),
             ),
             in_specs=[hbm, hbm],
-            out_specs=(vmem, vmem, vmem),
+            out_specs=(vmem, vmem, vmem, vmem),
             scratch_shapes=[
-                pltpu.VMEM((rows, depth), jnp.bfloat16),
+                pltpu.VMEM((rows - BOTTOM, depth), jnp.bfloat16),
                 pltpu.VMEM((rows - BOTTOM, depth), jnp.bfloat16),
                 pltpu.VMEM((depth, cols), jnp.bfloat16),
                 pltpu.VMEM((rows - BOTTOM, cols), jnp.float32),
+                dma,
                 dma,
                 dma,
                 dma((B_PARTS,)),
@@ -379,20 +388,20 @@
                 pltpu.VMEM((BOTTOM, depth), jnp.bfloat16),
                 pltpu.VMEM((BOTTOM, cols), jnp.float32),
             ),
-            in_specs=[hbm, vmem, vmem, vmem],
+            in_specs=[vmem, vmem, vmem, vmem],
             out_specs=(vmem, vmem, vmem),
             scratch_shapes=[
                 dma((len(SECOND),)),
                 dma((len(SECOND),)),
             ],
             compiler_params=params(collective_id=1, vmem_limit_bytes=16 * 1024 * 1024),
-        )(a_blk, token, b_far, low)
+        )(a_low, token, b_far, low)
         return pl.pallas_call(
             write_bottom,
             out_shape=c_type,
             in_specs=[hbm, vmem, vmem, vmem, vmem],
             out_specs=hbm,
-            scratch_shapes=[pltpu.VMEM((SECOND[-1][1], cols), jnp.bfloat16), dma, dma],
+            scratch_shapes=[pltpu.VMEM((SECOND[-1][1], cols), jnp.bfloat16), dma, dma((4,))],
             input_output_aliases={0: 0},
             compiler_params=pltpu.CompilerParams(vmem_limit_bytes=16 * 1024 * 1024),
         )(written, c_ready, a_far, low_total, b_far)

time: 93.9 us -> 93.9 us (level)
  no operation moved by 1% of the time
where the time goes in v5:
time: 93.9 us; the launch traced here: 93.7 us
  Pallas kernels  93.6 us (100%)
    pallas_call x1, Pallas kernels, local_mm(): pl.pallas_call(first_kernel, out_shape=(pltpu.VMEM((rows - BOTTOM, cols),...  78 us
    pallas_call x1, Pallas kernels, local_mm(): pl.pallas_call(second_kernel, out_shape=(pltpu.VMEM((SECOND[-1][0], cols)...  12.9 us

profile of v5, /device:TPU:1, one launch (start us, length us, event | category | flops | bytes accessed | tf_op | source)
XLA Modules:
  0.0 93.7 jit_solution(6428032627332680727)
XLA Ops:
  0.0 78.0 %shard_map.28 = (bf16[832,2048]{1,0:T(8,128)(2,1)S(1)}, bf16[2048,2048]{1,0:T(8,128)(2,1)S(1)}, f32[192,2048]{1,0:T(8,128)S(1)}, bf16[192,2048]{1,0:T(8,128)(2,1)S(1)}) custom-call(bf16[2048,2048]{1,0:T(8,128)(2,1)} %a_ref.1, bf16[2048,2048]{1,0:T(8,128)(2,1)} %b_ref.1), custom_call_target="tpu_custom_call" | custom-call | flops 17179869184 | bytes 50331648 | tf_op jit(solution)/shard_map/pallas_call | solution.py:346
  78.0 1.8 %shard_map.29 = (bf16[1024,2048]{1,0:T(8,128)(2,1)}, f32[8,128]{1,0:T(8,128)S(1)}) custom-call(bf16[832,2048]{1,0:T(8,128)(2,1)S(1)} %get-tuple-element.14.top_ref), custom_call_target="tpu_custom_call" | custom-call | tf_op jit(solution)/shard_map/pallas_call | solution.py:376
  79.8 12.9 %shard_map.30 = (bf16[128,2048]{1,0:T(8,128)(2,1)S(1)}, bf16[192,2048]{1,0:T(8,128)(2,1)S(1)}, f32[192,2048]{1,0:T(8,128)S(1)}) custom-call(bf16[192,2048]{1,0:T(8,128)(2,1)S(1)} %get-tuple-element.16.a_low, f32[8,128]{1,0:T(8,128)S(1)} %get-tuple-element.17.token_ref, bf16[2048,2048]{1,0:T(8,128)(2,1)S(1)} %get-tuple-element.18.b_far, ...), custom_call_target="tpu_custom_call" | custom-call | tf_op jit(solution)/shard_map/pallas_call | solution.py:384
  92.7 1.0 %shard_map.31 = bf16[1024,2048]{1,0:T(8,128)(2,1)} custom-call(bf16[1024,2048]{1,0:T(8,128)(2,1)} %get-tuple-element.15.half_ref, bf16[128,2048]{1,0:T(8,128)(2,1)S(1)} %get-tuple-element.20.ready_ref, bf16[192,2048]{1,0:T(8,128)(2,1)S(1)} %get-tuple-element.21.a_far, f32[192,2048]{1,0:T(8,128)S(1)} %get-tuple-element.22.total, ...), custom_call_target="tpu_custom_call", output_to_operand_aliasing={{}: (0, {})} | custom-call | tf_op jit(solution)/shard_map/pallas_call | solution.py:399

commit v6 on v5

--- a/solution.py
+++ b/solution.py
@@ -175,6 +175,11 @@
     a_sends[0].start()
     own_a.start()
     own_low.start()
+    for value, b_buf in enumerate((b_near, b_far)):
+
+        @pl.when(slot == value)
+        def _():
+            own_of_b(b_buf).start()
 
     @pl.when(row == 1)
     def _():
@@ -191,7 +196,16 @@
     def _():
         to_relay.start()
 
+    for value, (b_mine, b_other) in enumerate(((b_near, b_far), (b_far, b_near))):
+
+        @pl.when(slot == value)
+        def _():
+            for send in sends_of_b(b_other):
+                send.wait_recv()
+            own_of_b(b_mine).wait()
+
     own_a.wait()
+    own_low.wait()
     a_sends[1].start()
 
     @pl.when(jnp.logical_not(upper))
@@ -205,21 +219,6 @@
     def _():
         for send in a_sends[HOLD:]:
             send.start()
-
-    for value, b_buf in enumerate((b_near, b_far)):
-
-        @pl.when(slot == value)
-        def _():
-            own_of_b(b_buf).start()
-
-    own_low.wait()
-    for value, (b_mine, b_other) in enumerate(((b_near, b_far), (b_far, b_near))):
-
-        @pl.when(slot == value)
-        def _():
-            own_of_b(b_mine).wait()
-            for send in sends_of_b(b_other):
-                send.wait_recv()
 
     col_tiles = cols // TILE_N
     tile_m = top // 4

time: 93.9 us -> 93.8 us (level)
  no operation moved by 1% of the time
where the time goes in v6:
time: 93.8 us; the launch traced here: 93.7 us
  Pallas kernels  93.6 us (100%)
    pallas_call x1, Pallas kernels, local_mm(): pl.pallas_call(first_kernel, out_shape=(pltpu.VMEM((rows - BOTTOM, cols),...  78 us
    pallas_call x1, Pallas kernels, local_mm(): pl.pallas_call(second_kernel, out_shape=(pltpu.VMEM((SECOND[-1][0], cols)...  12.9 us

profile of v6, /device:TPU:1, one launch (start us, length us, event | category | flops | bytes accessed | tf_op | source)
XLA Modules:
  0.0 93.7 jit_solution(10237744178248245770)
XLA Ops:
  0.0 78.0 %shard_map.28 = (bf16[832,2048]{1,0:T(8,128)(2,1)S(1)}, bf16[2048,2048]{1,0:T(8,128)(2,1)S(1)}, f32[192,2048]{1,0:T(8,128)S(1)}, bf16[192,2048]{1,0:T(8,128)(2,1)S(1)}) custom-call(bf16[2048,2048]{1,0:T(8,128)(2,1)} %a_ref.1, bf16[2048,2048]{1,0:T(8,128)(2,1)} %b_ref.1), custom_call_target="tpu_custom_call" | custom-call | flops 17179869184 | bytes 50331648 | tf_op jit(solution)/shard_map/pallas_call | solution.py:345
  78.0 1.8 %shard_map.29 = (bf16[1024,2048]{1,0:T(8,128)(2,1)}, f32[8,128]{1,0:T(8,128)S(1)}) custom-call(bf16[832,2048]{1,0:T(8,128)(2,1)S(1)} %get-tuple-element.14.top_ref), custom_call_target="tpu_custom_call" | custom-call | tf_op jit(solution)/shard_map/pallas_call | solution.py:375
  79.8 12.9 %shard_map.30 = (bf16[128,2048]{1,0:T(8,128)(2,1)S(1)}, bf16[192,2048]{1,0:T(8,128)(2,1)S(1)}, f32[192,2048]{1,0:T(8,128)S(1)}) custom-call(bf16[192,2048]{1,0:T(8,128)(2,1)S(1)} %get-tuple-element.16.a_low, f32[8,128]{1,0:T(8,128)S(1)} %get-tuple-element.17.token_ref, bf16[2048,2048]{1,0:T(8,128)(2,1)S(1)} %get-tuple-element.18.b_far, ...), custom_call_target="tpu_custom_call" | custom-call | tf_op jit(solution)/shard_map/pallas_call | solution.py:383
  92.7 1.0 %shard_map.31 = bf16[1024,2048]{1,0:T(8,128)(2,1)} custom-call(bf16[1024,2048]{1,0:T(8,128)(2,1)} %get-tuple-element.15.half_ref, bf16[128,2048]{1,0:T(8,128)(2,1)S(1)} %get-tuple-element.20.ready_ref, bf16[192,2048]{1,0:T(8,128)(2,1)S(1)} %get-tuple-element.21.a_far, f32[192,2048]{1,0:T(8,128)S(1)} %get-tuple-element.22.total, ...), custom_call_target="tpu_custom_call", output_to_operand_aliasing={{}: (0, {})} | custom-call | tf_op jit(solution)/shard_map/pallas_call | solution.py:398

commit v7 on v6

--- a/solution.py
+++ b/solution.py
@@ -12,7 +12,8 @@
 FIRST = (
     (0, 256, 0, 2048),
     (256, 256, 0, 2048),
-    (632, 8, 0, 2048),
+    (632, 8, 0, 1792),
+    (632, 8, 1792, 256),
     (512, 120, 0, 2048),
     (640, 64, 0, 2048),
     (704, 128, 0, 512),
@@ -28,9 +29,9 @@
     (128, 64, 1792, 256),
 )
 AROUND = 2
-HOLD = 4
-TURN = 5
-B_PARTS = 4
+HOLD = 5
+TURN = 6
+B_PARTS = 1
 TILE_N = 256
 
 
@@ -251,9 +252,9 @@
                 a_sends[TURN].wait_send()
                 pl.semaphore_signal(turn_sem, inc=1, device_id=beside, device_id_type=MESH)
 
-        if idx == AROUND + 1:
+        if idx == AROUND + 2:
             piece = (piece[0], piece[1] + FIRST[AROUND][1], *piece[2:])
-        if idx != AROUND:
+        if idx not in (AROUND, AROUND + 1):
             multiply(piece, a_far, b_far, total, c_ref)
         if idx == 0:
 

time: 93.8 us -> 93.8 us (level)
  no operation moved by 1% of the time
where the time goes in v7:
time: 93.8 us; the launch traced here: 93.7 us
  Pallas kernels  93.7 us (100%)
    pallas_call x1, Pallas kernels, local_mm(): pl.pallas_call(first_kernel, out_shape=(pltpu.VMEM((rows - BOTTOM, cols),...  78.1 us
    pallas_call x1, Pallas kernels, local_mm(): pl.pallas_call(second_kernel, out_shape=(pltpu.VMEM((SECOND[-1][0], cols)...  12.9 us

profile of v7, /device:TPU:1, one launch (start us, length us, event | category | flops | bytes accessed | tf_op | source)
XLA Modules:
  0.0 93.7 jit_solution(14451516219965500748)
XLA Ops:
  0.0 78.1 %shard_map.28 = (bf16[832,2048]{1,0:T(8,128)(2,1)S(1)}, bf16[2048,2048]{1,0:T(8,128)(2,1)S(1)}, f32[192,2048]{1,0:T(8,128)S(1)}, bf16[192,2048]{1,0:T(8,128)(2,1)S(1)}) custom-call(bf16[2048,2048]{1,0:T(8,128)(2,1)} %a_ref.1, bf16[2048,2048]{1,0:T(8,128)(2,1)} %b_ref.1), custom_call_target="tpu_custom_call" | custom-call | flops 17179869184 | bytes 50331648 | tf_op jit(solution)/shard_map/pallas_call | solution.py:346
  78.1 1.8 %shard_map.29 = (bf16[1024,2048]{1,0:T(8,128)(2,1)}, f32[8,128]{1,0:T(8,128)S(1)}) custom-call(bf16[832,2048]{1,0:T(8,128)(2,1)S(1)} %get-tuple-element.14.top_ref), custom_call_target="tpu_custom_call" | custom-call | tf_op jit(solution)/shard_map/pallas_call | solution.py:376
  79.8 12.9 %shard_map.30 = (bf16[128,2048]{1,0:T(8,128)(2,1)S(1)}, bf16[192,2048]{1,0:T(8,128)(2,1)S(1)}, f32[192,2048]{1,0:T(8,128)S(1)}) custom-call(bf16[192,2048]{1,0:T(8,128)(2,1)S(1)} %get-tuple-element.16.a_low, f32[8,128]{1,0:T(8,128)S(1)} %get-tuple-element.17.token_ref, bf16[2048,2048]{1,0:T(8,128)(2,1)S(1)} %get-tuple-element.18.b_far, ...), custom_call_target="tpu_custom_call" | custom-call | tf_op jit(solution)/shard_map/pallas_call | solution.py:384
  92.7 1.0 %shard_map.31 = bf16[1024,2048]{1,0:T(8,128)(2,1)} custom-call(bf16[1024,2048]{1,0:T(8,128)(2,1)} %get-tuple-element.15.half_ref, bf16[128,2048]{1,0:T(8,128)(2,1)S(1)} %get-tuple-element.20.ready_ref, bf16[192,2048]{1,0:T(8,128)(2,1)S(1)} %get-tuple-element.21.a_far, f32[192,2048]{1,0:T(8,128)S(1)} %get-tuple-element.22.total, ...), custom_call_target="tpu_custom_call", output_to_operand_aliasing={{}: (0, {})} | custom-call | tf_op jit(solution)/shard_map/pallas_call | solution.py:399

commit v8 on v7

--- a/solution.py
+++ b/solution.py
@@ -10,8 +10,8 @@
 MESH = pl.DeviceIdType.MESH
 BOTTOM = 192
 FIRST = (
-    (0, 256, 0, 2048),
-    (256, 256, 0, 2048),
+    (0, 128, 0, 2048),
+    (128, 384, 0, 2048),
     (632, 8, 0, 1792),
     (632, 8, 1792, 256),
     (512, 120, 0, 2048),
@@ -31,7 +31,6 @@
 AROUND = 2
 HOLD = 5
 TURN = 6
-B_PARTS = 1
 TILE_N = 256
 
 
@@ -133,8 +132,8 @@
         pl.semaphore_signal(ready_sem, inc=1, device_id=beside, device_id_type=MESH)
 
     a_sends = sends_of(FIRST, a_own, a_far, asend_sem, arecv_sem, across)
-    first_rows = a_ref.at[pl.ds(base, FIRST[0][1]), :]
-    a_sends[0] = sends_of(FIRST[:1], first_rows, a_far, asend_sem, arecv_sem, across)[0]
+    first_rows = a_ref.at[pl.ds(base, top), :]
+    a_sends[:AROUND] = sends_of(FIRST[:AROUND], first_rows, a_far, asend_sem, arecv_sem, across)
     r0, nr, k0, nk = FIRST[AROUND]
     to_relay = pltpu.make_async_remote_copy(
         src_ref=a_ref.at[pl.ds(r0, nr), pl.ds(k0, nk)],
@@ -152,28 +151,31 @@
         device_id=below,
         device_id_type=MESH,
     )
-    part = depth // B_PARTS
-
-    def sends_of_b(b_buf):
-        return [
-            pltpu.make_async_remote_copy(
-                src_ref=b_ref.at[pl.ds(idx * part, part), :],
-                dst_ref=b_buf.at[pl.ds(idx * part, part), :],
-                send_sem=bsend_sem.at[idx],
-                recv_sem=brecv_sem.at[idx],
-                device_id=beside,
-                device_id_type=MESH,
-            )
-            for idx in range(B_PARTS)
-        ]
+    own_a = pltpu.make_async_copy(a_ref.at[pl.ds(base, top), :], a_own, own_sem)
+    own_low = pltpu.make_async_copy(a_ref.at[pl.ds(base + top, bottom), :], a_low, low_sem)
 
     def own_of_b(b_buf):
         return pltpu.make_async_copy(b_ref, b_buf, bown_sem)
 
-    own_a = pltpu.make_async_copy(a_ref.at[pl.ds(base, top), :], a_own, own_sem)
-    own_low = pltpu.make_async_copy(a_ref.at[pl.ds(base + top, bottom), :], a_low, low_sem)
+    def send_of_b(b_buf):
+        return pltpu.make_async_remote_copy(
+            src_ref=b_buf,
+            dst_ref=b_buf,
+            send_sem=bsend_sem,
+            recv_sem=brecv_sem,
+            device_id=beside,
+            device_id_type=MESH,
+        )
 
     a_sends[0].start()
+
+    @pl.when(lower)
+    def _():
+        to_relay.start()
+
+    for send in a_sends[1:AROUND]:
+        send.start()
+
     own_a.start()
     own_low.start()
     for value, b_buf in enumerate((b_near, b_far)):
@@ -186,40 +188,38 @@
     def _():
         pl.semaphore_wait(ready_sem, 1)
 
+    a_sends[0].wait_recv()
+    own_a.wait()
+    own_low.wait()
     for value, b_buf in enumerate((b_near, b_far)):
 
         @pl.when(slot == value)
         def _():
-            for send in sends_of_b(b_buf):
-                send.start()
+            own_of_b(b_buf).wait()
+            send_of_b(b_buf).start()
+
+    @pl.when(jnp.logical_not(upper))
+    def _():
+        a_sends[AROUND].start()
+
+    for send in a_sends[AROUND + 1 : HOLD]:
+        send.start()
+
+    @pl.when(row == 0)
+    def _():
+        for send in a_sends[HOLD:]:
+            send.start()
 
     @pl.when(lower)
     def _():
-        to_relay.start()
-
-    for value, (b_mine, b_other) in enumerate(((b_near, b_far), (b_far, b_near))):
+        to_relay.wait_recv()
+        from_relay.start()
+
+    for value, b_buf in enumerate((b_far, b_near)):
 
         @pl.when(slot == value)
         def _():
-            for send in sends_of_b(b_other):
-                send.wait_recv()
-            own_of_b(b_mine).wait()
-
-    own_a.wait()
-    own_low.wait()
-    a_sends[1].start()
-
-    @pl.when(jnp.logical_not(upper))
-    def _():
-        a_sends[AROUND].start()
-
-    for send in a_sends[AROUND + 1 : HOLD]:
-        send.start()
-
-    @pl.when(row == 0)
-    def _():
-        for send in a_sends[HOLD:]:
-            send.start()
+            send_of_b(b_buf).wait_recv()
 
     col_tiles = cols // TILE_N
     tile_m = top // 4
@@ -244,7 +244,8 @@
                 for send in a_sends[HOLD:]:
                     send.start()
 
-        a_sends[idx].wait_recv()
+        if idx:
+            a_sends[idx].wait_recv()
         if idx == TURN:
 
             @pl.when(row == 0)
@@ -256,13 +257,6 @@
             piece = (piece[0], piece[1] + FIRST[AROUND][1], *piece[2:])
         if idx not in (AROUND, AROUND + 1):
             multiply(piece, a_far, b_far, total, c_ref)
-        if idx == 0:
-
-            @pl.when(lower)
-            def _():
-                to_relay.wait_recv()
-                from_relay.start()
-
     for idx, send in enumerate(a_sends):
         if idx not in (TURN, AROUND):
             send.wait_send()
@@ -284,8 +278,7 @@
 
         @pl.when(slot == value)
         def _():
-            for send in sends_of_b(b_buf):
-                send.wait_send()
+            send_of_b(b_buf).wait_send()
 
 
 def second_kernel(a_low, token_ref, b_far, low_ref, c_ref, a_far, total, asend_sem, arecv_sem):
@@ -361,8 +354,8 @@
                 dma,
                 dma,
                 dma,
-                dma((B_PARTS,)),
-                dma((B_PARTS,)),
+                dma,
+                dma,
                 dma((len(FIRST),)),
                 dma((len(FIRST),)),
                 pltpu.SemaphoreType.REGULAR,

time: 93.8 us -> 93.8 us (level)
  no operation moved by 1% of the time
where the time goes in v8:
time: 93.8 us; the launch traced here: 93.7 us
  Pallas kernels  93.7 us (100%)
    pallas_call x1, Pallas kernels, local_mm(): pl.pallas_call(first_kernel, out_shape=(pltpu.VMEM((rows - BOTTOM, cols),...  78.1 us
    pallas_call x1, Pallas kernels, local_mm(): pl.pallas_call(second_kernel, out_shape=(pltpu.VMEM((SECOND[-1][0], cols)...  12.9 us

profile of v8, /device:TPU:1, one launch (start us, length us, event | category | flops | bytes accessed | tf_op | source)
XLA Modules:
  0.0 93.7 jit_solution(4477892553990091020)
XLA Ops:
  0.0 78.1 %shard_map.28 = (bf16[832,2048]{1,0:T(8,128)(2,1)S(1)}, bf16[2048,2048]{1,0:T(8,128)(2,1)S(1)}, f32[192,2048]{1,0:T(8,128)S(1)}, bf16[192,2048]{1,0:T(8,128)(2,1)S(1)}) custom-call(bf16[2048,2048]{1,0:T(8,128)(2,1)} %a_ref.1, bf16[2048,2048]{1,0:T(8,128)(2,1)} %b_ref.1), custom_call_target="tpu_custom_call" | custom-call | flops 17179869184 | bytes 50331648 | tf_op jit(solution)/shard_map/pallas_call | solution.py:339
  78.1 1.8 %shard_map.29 = (bf16[1024,2048]{1,0:T(8,128)(2,1)}, f32[8,128]{1,0:T(8,128)S(1)}) custom-call(bf16[832,2048]{1,0:T(8,128)(2,1)S(1)} %get-tuple-element.14.top_ref), custom_call_target="tpu_custom_call" | custom-call | tf_op jit(solution)/shard_map/pallas_call | solution.py:369
  79.8 12.9 %shard_map.30 = (bf16[128,2048]{1,0:T(8,128)(2,1)S(1)}, bf16[192,2048]{1,0:T(8,128)(2,1)S(1)}, f32[192,2048]{1,0:T(8,128)S(1)}) custom-call(bf16[192,2048]{1,0:T(8,128)(2,1)S(1)} %get-tuple-element.16.a_low, f32[8,128]{1,0:T(8,128)S(1)} %get-tuple-element.17.token_ref, bf16[2048,2048]{1,0:T(8,128)(2,1)S(1)} %get-tuple-element.18.b_far, ...), custom_call_target="tpu_custom_call" | custom-call | tf_op jit(solution)/shard_map/pallas_call | solution.py:377
  92.7 1.0 %shard_map.31 = bf16[1024,2048]{1,0:T(8,128)(2,1)} custom-call(bf16[1024,2048]{1,0:T(8,128)(2,1)} %get-tuple-element.15.half_ref, bf16[128,2048]{1,0:T(8,128)(2,1)S(1)} %get-tuple-element.20.ready_ref, bf16[192,2048]{1,0:T(8,128)(2,1)S(1)} %get-tuple-element.21.a_far, f32[192,2048]{1,0:T(8,128)S(1)} %get-tuple-element.22.total, ...), custom_call_target="tpu_custom_call", output_to_operand_aliasing={{}: (0, {})} | custom-call | tf_op jit(solution)/shard_map/pallas_call | solution.py:392

commit v9 on v8

--- a/solution.py
+++ b/solution.py
@@ -12,12 +12,11 @@
 FIRST = (
     (0, 128, 0, 2048),
     (128, 384, 0, 2048),
-    (632, 8, 0, 1792),
-    (632, 8, 1792, 256),
-    (512, 120, 0, 2048),
-    (640, 64, 0, 2048),
-    (704, 128, 0, 512),
-    (704, 128, 512, 512),
+    (584, 8, 0, 1664),
+    (584, 8, 1664, 384),
+    (512, 72, 0, 2048),
+    (592, 112, 0, 2048),
+    (704, 128, 0, 1024),
     (704, 128, 1024, 512),
     (704, 128, 1536, 512),
 )
@@ -30,7 +29,7 @@
 )
 AROUND = 2
 HOLD = 5
-TURN = 6
+TURN = 5
 TILE_N = 256
 
 

time: 93.8 us -> 93.8 us (level)
  no operation moved by 1% of the time
where the time goes in v9:
time: 93.8 us; the launch traced here: 93.7 us
  Pallas kernels  93.6 us (100%)
    pallas_call x1, Pallas kernels, local_mm(): pl.pallas_call(first_kernel, out_shape=(pltpu.VMEM((rows - BOTTOM, cols),...  77.5 us
    pallas_call x1, Pallas kernels, local_mm(): pl.pallas_call(second_kernel, out_shape=(pltpu.VMEM((SECOND[-1][0], cols)...  13.4 us

profile of v9, /device:TPU:1, one launch (start us, length us, event | category | flops | bytes accessed | tf_op | source)
XLA Modules:
  0.0 93.7 jit_solution(620403843103541899)
XLA Ops:
  0.0 77.5 %shard_map.28 = (bf16[832,2048]{1,0:T(8,128)(2,1)S(1)}, bf16[2048,2048]{1,0:T(8,128)(2,1)S(1)}, f32[192,2048]{1,0:T(8,128)S(1)}, bf16[192,2048]{1,0:T(8,128)(2,1)S(1)}) custom-call(bf16[2048,2048]{1,0:T(8,128)(2,1)} %a_ref.1, bf16[2048,2048]{1,0:T(8,128)(2,1)} %b_ref.1), custom_call_target="tpu_custom_call" | custom-call | flops 17179869184 | bytes 50331648 | tf_op jit(solution)/shard_map/pallas_call | solution.py:338
  77.5 1.8 %shard_map.29 = (bf16[1024,2048]{1,0:T(8,128)(2,1)}, f32[8,128]{1,0:T(8,128)S(1)}) custom-call(bf16[832,2048]{1,0:T(8,128)(2,1)S(1)} %get-tuple-element.14.top_ref), custom_call_target="tpu_custom_call" | custom-call | tf_op jit(solution)/shard_map/pallas_call | solution.py:368
  79.3 13.4 %shard_map.30 = (bf16[128,2048]{1,0:T(8,128)(2,1)S(1)}, bf16[192,2048]{1,0:T(8,128)(2,1)S(1)}, f32[192,2048]{1,0:T(8,128)S(1)}) custom-call(bf16[192,2048]{1,0:T(8,128)(2,1)S(1)} %get-tuple-element.16.a_low, f32[8,128]{1,0:T(8,128)S(1)} %get-tuple-element.17.token_ref, bf16[2048,2048]{1,0:T(8,128)(2,1)S(1)} %get-tuple-element.18.b_far, ...), custom_call_target="tpu_custom_call" | custom-call | tf_op jit(solution)/shard_map/pallas_call | solution.py:376
  92.7 1.0 %shard_map.31 = bf16[1024,2048]{1,0:T(8,128)(2,1)} custom-call(bf16[1024,2048]{1,0:T(8,128)(2,1)} %get-tuple-element.15.half_ref, bf16[128,2048]{1,0:T(8,128)(2,1)S(1)} %get-tuple-element.20.ready_ref, bf16[192,2048]{1,0:T(8,128)(2,1)S(1)} %get-tuple-element.21.a_far, f32[192,2048]{1,0:T(8,128)S(1)} %get-tuple-element.22.total, ...), custom_call_target="tpu_custom_call", output_to_operand_aliasing={{}: (0, {})} | custom-call | tf_op jit(solution)/shard_map/pallas_call | solution.py:391
